TPU v7x, 32 devices: a whole 2x2x4 slice. The times are simulated.
32 devices in a mesh: seq: 8 (over z, y), tp: 4 (over x, core).
Axes of the slice: x: 2, y: 2, z: 4, core: 2. Of those that a mesh axis runs over, the one named last changes fastest.
Arguments:
- encoded: bfloat16 [8192, 1280], P(('seq', 'tp')), may hold values from -6 to 6
- starts: int32 [32, 32], replicated, may hold values from 0 to 256, as said below
- w_up: bfloat16 [1280, 4096], P(None, 'tp'), may hold values from -0.15625 to 0.15625
- norm_gain: float32 [4096], replicated, may hold values from 0.25 to 1.75
- w_query: bfloat16 [4096, 4096], P(None, 'tp'), may hold values from -8 to 8
- w_key: bfloat16 [4096, 4096], P(None, 'tp'), may hold values from -8 to 8
- w_value: bfloat16 [4096, 4096], P(None, 'tp'), may hold values from -0.09375 to 0.09375
- w_out: bfloat16 [4096, 4096], P('tp'), may hold values from -0.09375 to 0.09375
- cotangent: bfloat16 [1024, 4096], P('seq', 'tp'), may hold values from -6 to 6
Outputs:
- latent_out: bfloat16 [1024, 4096], P('seq', 'tp')
- latent_grad: float32 [1024, 4096], P('seq', 'tp')
Inputs may be any that keep to these rules, and one draw needn't show every extreme that they name: `starts`: row i lists in increasing order the distinct offsets at which patches begin in byte shard i, followed by 256 in unused slots; every shard has at least one patch and at least 8, some shard exactly 32; shard 0 begins a patch at offset 0.
All inputs are finite; a program needn't handle non-finite values.
Results may differ from a plain program's by a relative error of at most 0.014.
Values may be sent and summed in bfloat16 or wider, within the bound.
A program may use at most 128 MiB of HBM per device.

v0:
```python
import jax
import jax.numpy as jnp
from jax import lax
from jax.sharding import PartitionSpec as P

HEAD_DIM = 128


EPS = 1e-05
NEG = -1e30
CONTRACT_LAST = (((1,), (1,)), ((), ()))


def shifted(block, axis, distance):
    devices = range(lax.axis_size(axis))
    route = [(i - distance, i) for i in devices if i - distance in devices]
    return lax.ppermute(block, axis, route)


def per_device(encoded, starts, w_up, norm_gain, w_query, w_key, w_value, w_out, cotangent):
    byte_rows = encoded.shape[0]
    patch_cap = starts.shape[1]
    model_width = norm_gain.shape[0]
    shard = lax.axis_index(("seq", "tp"))
    own_starts = lax.dynamic_slice_in_dim(starts, shard, 1, 0)[0]
    places = jnp.arange(byte_rows, dtype=jnp.int32)
    following = jnp.concatenate([own_starts[1:], jnp.full((1,), byte_rows, jnp.int32)])
    inside = (places[None, :] >= own_starts[:, None]) & (places[None, :] < following[:, None])
    sums = jnp.dot(inside.astype(jnp.bfloat16), encoded, preferred_element_type=jnp.float32)
    sizes = jnp.sum(inside.astype(jnp.float32), 1)
    leading = places[None, :] < own_starts[:1, None]
    lead_sum = jnp.dot(leading.astype(jnp.bfloat16), encoded, preferred_element_type=jnp.float32)
    lead_size = jnp.sum(leading.astype(jnp.float32), 1)
    next_sum, next_size = shifted((lead_sum, lead_size), ("seq", "tp"), -1)
    count = jnp.sum((own_starts < byte_rows).astype(jnp.int32))
    last_slot = (jnp.arange(patch_cap, dtype=jnp.int32) == count - 1).astype(jnp.float32)
    sums = sums + last_slot[:, None] * next_sum
    sizes = sizes + last_slot * next_size
    patches = (sums / jnp.maximum(sizes, 1.0)[:, None]).astype(jnp.bfloat16)
    group = lax.all_gather(patches, "tp", axis=0, tiled=True)
    latent_in = jnp.dot(group, w_up, preferred_element_type=jnp.float32).astype(jnp.bfloat16)
    group_rows, columns = latent_in.shape
    head_count = columns // HEAD_DIM
    wide_piece = lax.all_gather(latent_in, "tp", axis=1, tiled=True).astype(jnp.float32)
    scaled = (wide_piece * norm_gain[None, :]).astype(jnp.bfloat16)
    acc_query = jnp.dot(scaled, w_query, preferred_element_type=jnp.float32)
    acc_key = jnp.dot(scaled, w_key, preferred_element_type=jnp.float32)
    acc_value = jnp.dot(scaled, w_value, preferred_element_type=jnp.float32)
    acc_query, acc_key, acc_value, square = (
        acc_query,
        acc_key,
        acc_value,
        jnp.sum(wide_piece * wide_piece, 1),
    )
    rinv = lax.rsqrt(square / model_width + EPS)
    query = (rinv[:, None] * acc_query).astype(jnp.bfloat16)
    key_rows = (rinv[:, None] * acc_key).astype(jnp.bfloat16)
    value_rows = (rinv[:, None] * acc_value).astype(jnp.bfloat16)
    keys_all, values_all = (
        lax.all_gather(key_rows, "seq", axis=0, tiled=True),
        lax.all_gather(value_rows, "seq", axis=0, tiled=True),
    )
    patches_total = keys_all.shape[0]
    valid_all = (starts < byte_rows).reshape(patches_total)
    row_base = lax.axis_index("seq") * group_rows
    query_index = row_base + jnp.arange(group_rows, dtype=jnp.int32)
    key_index = jnp.arange(patches_total, dtype=jnp.int32)
    query_valid = lax.dynamic_slice_in_dim(valid_all, row_base, group_rows, 0)
    allowed = valid_all[None, :] & (key_index[None, :] <= query_index[:, None])
    scale = HEAD_DIM ** (-0.5)
    query_heads = query.reshape(group_rows, head_count, HEAD_DIM)
    key_heads = keys_all.reshape(patches_total, head_count, HEAD_DIM)
    value_heads = values_all.reshape(patches_total, head_count, HEAD_DIM)
    scores = (
        jnp.einsum("rhd,khd->hrk", query_heads, key_heads, preferred_element_type=jnp.float32)
        * scale
    )
    peak = jnp.max(jnp.where(allowed[None], scores, NEG), 2)
    expo = jnp.where(allowed[None], jnp.exp(scores - peak[:, :, None]), 0.0)
    total = jnp.sum(expo, 2)
    mixed = jnp.einsum(
        "hrk,khd->rhd", expo.astype(jnp.bfloat16), value_heads, preferred_element_type=jnp.float32
    )
    attn = (mixed / total.T[:, :, None]).astype(jnp.bfloat16)
    partial_value = jnp.dot(
        attn.reshape(group_rows, columns), w_out, preferred_element_type=jnp.float32
    )
    head_sum = lax.psum_scatter(
        partial_value.astype(jnp.bfloat16), "tp", scatter_dimension=1, tiled=True
    ).astype(jnp.float32)
    wide_in = latent_in.astype(jnp.float32)
    latent_out = jnp.where(query_valid[:, None], wide_in + head_sum, 0.0).astype(jnp.bfloat16)
    grad_out = jnp.where(query_valid[:, None], cotangent, jnp.zeros_like(cotangent))
    d_attn = lax.dot_general(
        lax.all_gather(grad_out, "tp", axis=1, tiled=True),
        w_out,
        CONTRACT_LAST,
        preferred_element_type=jnp.float32,
    ).astype(jnp.bfloat16)
    grad_heads = d_attn.reshape(group_rows, head_count, HEAD_DIM)
    delta = jnp.sum(grad_heads.astype(jnp.float32) * attn.astype(jnp.float32), 2).T
    probs = expo / total[:, :, None]
    d_probs = jnp.einsum(
        "rhd,khd->hrk", grad_heads, value_heads, preferred_element_type=jnp.float32
    )
    d_scores = (probs * (d_probs - delta[:, :, None])).astype(jnp.bfloat16)
    grad_query = (
        (
            jnp.einsum("hrk,khd->rhd", d_scores, key_heads, preferred_element_type=jnp.float32)
            * scale
        )
        .astype(jnp.bfloat16)
        .reshape(group_rows, columns)
    )
    weights_low = probs.astype(jnp.bfloat16)
    count_rows = group_rows * lax.axis_size("seq")
    key_part = jnp.einsum("hrk,rhd->khd", d_scores, query_heads, preferred_element_type=jnp.float32)
    value_part = jnp.einsum(
        "hrk,rhd->khd", weights_low, grad_heads, preferred_element_type=jnp.float32
    )
    both = lax.psum_scatter(
        jnp.concatenate(
            [key_part.reshape(count_rows, columns), value_part.reshape(count_rows, columns)], 1
        ).astype(jnp.bfloat16),
        "seq",
        scatter_dimension=0,
        tiled=True,
    ).astype(jnp.float32)
    grad_key = (both[:, :columns] * scale).astype(jnp.bfloat16)
    grad_value = both[:, columns:].astype(jnp.bfloat16)
    dnormed = (
        lax.dot_general(grad_query, w_query, CONTRACT_LAST, preferred_element_type=jnp.float32)
        + lax.dot_general(grad_key, w_key, CONTRACT_LAST, preferred_element_type=jnp.float32)
        + lax.dot_general(grad_value, w_value, CONTRACT_LAST, preferred_element_type=jnp.float32)
    )
    normed_grad = lax.psum_scatter(
        dnormed.astype(jnp.bfloat16), "tp", scatter_dimension=1, tiled=True
    ).astype(jnp.float32)
    gain_own = lax.dynamic_slice_in_dim(norm_gain, lax.axis_index("tp") * columns, columns, 0)
    dots = lax.psum(jnp.sum(gain_own[None, :] * normed_grad * wide_in, 1), "tp")
    latent_grad = (
        grad_out.astype(jnp.float32)
        + rinv[:, None] * gain_own[None, :] * normed_grad
        - wide_in * (rinv**3)[:, None] * dots[:, None] / model_width
    )
    return (latent_out, latent_grad)


def solution(mesh):
    in_specs = (
        P(("seq", "tp"), None),
        P(),
        P(None, "tp"),
        P(),
        P(None, "tp"),
        P(None, "tp"),
        P(None, "tp"),
        P("tp", None),
        P("seq", "tp"),
    )
    out_specs = (P("seq", "tp"), P("seq", "tp"))
    return jax.shard_map(
        per_device, mesh=mesh, in_specs=in_specs, out_specs=out_specs, check_vma=False
    )
```

profile of v0, /device:TPU:0, one launch (start us, length us, event | category | flops | bytes accessed | tf_op | source)
XLA Modules:
  0.0 346.3 jit_solution(8448537527202758560)
XLA Ops:
  7.2 1.5 fusion.66
  8.7 0.6 fusion.63
  9.4 1.3 collective-permute-start.1
  10.7 1.3 fusion.71
  12.0 1.4 collective-permute-start
  14.2 0.2 convert_reduce_fusion
  14.4 0.6 fusion.65
  15.1 0.7 collective-permute-done
  15.8 1.4 divide_convert_fusion
  17.2 10.4 %all_gather.15 = bf16[128,1280]{1,0:T(8,128)(2,1)S(1)} all-gather(bf16[32,1280]{1,0:T(8,128)(2,1)S(1)} %divide_convert_fusion), channel_id=1, replica_groups=mesh['seq'=8,'tp'=4] {'tp'}, dimensions={0}, use_global_device_ids=true | all-gather | bytes 409600 | tf_op jit(solution)/shard_map/all_gather | solution.py:40
  27.6 1.2 convolution_convert_fusion.3
  29.1 0.8 broadcast_select_fusion
  29.9 15.9 %all-gather.5.cloned.1.call-done = bf16[128,4096]{1,0:T(8,128)(2,1)} async-done(((bf16[128,1024]{1,0:T(8,128)(2,1)}), bf16[128,4096]{1,0:T(8,128)(2,1)}) %all-gather.5.cloned.1.call-update) | async-done | bytes 1048592 | tf_op jit(solution)/shard_map/all_gather | solution.py:44
  45.9 1.5 fusion.6
  47.4 5.7 %fusion.29 = bf16[128,1024]{1,0:T(8,128)(2,1)} fusion(bf16[4096,1024]{1,0:T(8,128)(2,1)} %param.14, bf16[128,4096]{1,0:T(8,128)(2,1)} %all-gather.5.cloned.1.call-done, f32[4096]{0:T(1024)S(1)} %copy-done.9, f32[128]{0:T(128)S(1)} %get-tuple-element.7), kind=kOutput, calls=%fused_computation.36 | convolution fusion | flops 1075576832 | bytes 9716224 | tf_op jit(solution)/shard_map/dot_general | solution.py:47
  53.3 5.6 %fusion.27 = bf16[128,1024]{1,0:T(8,128)(2,1)} fusion(bf16[4096,1024]{1,0:T(8,128)(2,1)} %param.15, bf16[128,4096]{1,0:T(8,128)(2,1)S(1)} %copy-done.2, f32[4096]{0:T(1024)S(1)} %copy-done.9, f32[128]{0:T(128)S(1)} %get-tuple-element.7), kind=kOutput, calls=%fused_computation.34 | convolution fusion | flops 1075576832 | bytes 9716224 | tf_op jit(solution)/shard_map/dot_general | solution.py:48
  58.9 0.2 reduce-scatter.10.cloned.1.call-start
  59.3 4.9 %all-gather.11.cloned.1.call-done = bf16[128,4096]{1,0:T(8,128)(2,1)} async-done(((bf16[128,1024]{1,0:T(8,128)(2,1)}), bf16[128,4096]{1,0:T(8,128)(2,1)}) %all-gather.11.cloned.1.call-update) | async-done | bytes 1048592 | tf_op jit(solution)/shard_map/all_gather | solution.py:95
  64.2 6.6 %convolution_convert_fusion.2 = bf16[128,1024]{1,0:T(8,128)(2,1)S(1)} fusion(bf16[128,4096]{1,0:T(8,128)(2,1)} %all-gather.11.cloned.1.call-done, bf16[1024,4096]{1,0:T(8,128)(2,1)} %param.16), kind=kOutput, calls=%fused_computation.37 | convolution fusion | flops 1073872896 | bytes 9699328 | tf_op jit(solution)/shard_map/dot_general | solution.py:94
  70.8 0.2 copy.30
  71.0 4.7 %fusion.28 = bf16[128,1024]{1,0:T(8,128)(2,1)S(1)} fusion(bf16[4096,1024]{1,0:T(8,128)(2,1)} %param.13, bf16[128,4096]{1,0:T(8,128)(2,1)S(1)} %copy-done.2, f32[4096]{0:T(1024)S(1)} %copy-done.9, f32[128]{0:T(128)S(1)} %get-tuple-element.7), kind=kOutput, calls=%fused_computation.35 | convolution fusion | flops 1075576832 | bytes 9716224 | tf_op jit(solution)/shard_map/dot_general | solution.py:46
  75.7 0.2 copy.40
  75.8 40.2 %all-gather.9.cloned.1.call-done = bf16[1024,1024]{1,0:T(8,128)(2,1)} async-done(((bf16[128,1024]{1,0:T(8,128)(2,1)}), bf16[1024,1024]{1,0:T(8,128)(2,1)}) %all-gather.9.cloned.1.call-update) | async-done | bytes 2097168 | tf_op jit(solution)/shard_map/all_gather | solution.py:60
  116.0 2.9 copy.41
  118.9 4.2 %fusion.70 = (f32[8,128]{1,0:T(8,128)S(1)}, f32[8,128,1024]{2,1,0:T(8,128)}) fusion(pred[128,1024]{1,0:T(8,128)(4,1)S(1)} %fusion.51, bf16[128,8,128]{0,2,1:T(8,128)(2,1)S(1)} %bitcast.82, bf16[1024,8,128]{0,2,1:T(8,128)(2,1)S(1)} %bitcast.77), kind=kOutput, calls=%fused_computation.89 | convolution fusion | flops 543163392 | bytes 6688768 | tf_op jit(solution)/shard_map/sub | solution.py:79
  123.1 4.4 %fusion.17 = bf16[8,128,1024]{2,1,0:T(8,128)(2,1)} fusion(bf16[128,8,128]{0,2,1:T(8,128)(2,1)S(1)} %bitcast.84, f32[8,128,1024]{2,1,0:T(8,128)} %get-tuple-element.9, f32[8,128]{1,0:T(8,128)S(1)} %get-tuple-element.8), kind=kOutput, calls=%fused_computation.25 | convolution fusion | flops 271581184 | bytes 6557696 | tf_op jit(solution)/shard_map/hrk,rhd->khd/dot_general | solution.py:118
  127.6 38.1 %all-gather.7.cloned.1.call-done = bf16[1024,1024]{1,0:T(8,128)(2,1)} async-done(((bf16[128,1024]{1,0:T(8,128)(2,1)}), bf16[1024,1024]{1,0:T(8,128)(2,1)}) %all-gather.7.cloned.1.call-update) | async-done | bytes 2097168 | tf_op jit(solution)/shard_map/all_gather | solution.py:61
  165.7 4.0 %multiply_reduce_fusion = (f32[128,8]{0,1:T(8,128)S(1)}, bf16[128,8,128]{0,2,1:T(8,128)(2,1)S(1)}) fusion(bf16[128,1024]{0,1:T(8,128)(2,1)S(1)} %copy.30, f32[128,8]{0,1:T(8,128)S(1)} %bitcast.87, f32[8,128,1024]{2,1,0:T(8,128)} %get-tuple-element.9, bf16[1024,1024]{1,0:T(8,128)(2,1)} %all-gather.7.cloned.1.call-done), kind=kOutput, calls=%fused_computation.55 | convolution fusion | flops 270269440 | bytes 6823936 | tf_op jit(solution)/shard_map/hrk,khd->rhd/dot_general | solution.py:81
  169.7 0.7 copy-done.6
  170.4 1.2 multiply_convert_fusion
  171.6 1.4 copy-done.3
  173.0 0.7 convolution_convert_fusion.1
  173.7 0.9 copy-done.7
  174.6 2.4 pad_maximum_fusion
  177.0 6.5 %copy.36 = bf16[1024,2048]{1,0:T(8,128)(2,1)} copy(bf16[1024,2048]{0,1:T(8,128)(2,1)} %pad_maximum_fusion) | data formatting | bytes 8388608
  183.5 0.3 reduce-scatter.8.cloned.1.call-start
  183.8 2.3 fusion.30
  186.1 6.4 %fusion.72 = f32[128,4096]{1,0:T(8,128)S(1)} fusion(bf16[128,1024]{0,1:T(8,128)(2,1)S(1)} %bitcast.86, bf16[4096,1024]{1,0:T(8,128)(2,1)} %param.13), kind=kOutput, calls=%fused_computation.91 | convolution fusion | flops 1073741824 | bytes 10747904 | tf_op jit(solution)/shard_map/dot_general | solution.py:132
  192.4 78.1 %reduce-scatter.10.cloned.1.call-done = bf16[128,2048]{1,0:T(8,128)(2,1)} async-done(((bf16[1024,2048]{1,0:T(8,128)(2,1)}), bf16[128,2048]{1,0:T(8,128)(2,1)}) %reduce-scatter.10.cloned.1.call-update) | async-done | bytes 524304
  270.5 1.0 slice.26
  271.7 6.4 %convolution_add_fusion.1 = f32[128,4096]{1,0:T(8,128)S(1)} fusion(f32[128,4096]{1,0:T(8,128)S(1)} %fusion.72, bf16[4096,1024]{1,0:T(8,128)(2,1)} %param.14, bf16[128,1024]{0,1:T(8,128)(2,1)S(1)} %copy.38), kind=kOutput, calls=%fused_computation.2 | convolution fusion | flops 1074659328 | bytes 12845056 | tf_op jit(solution)/shard_map/dot_general | solution.py:133
  278.1 7.2 %fusion.1 = bf16[128,4096]{1,0:T(8,128)(2,1)} fusion(f32[128,4096]{1,0:T(8,128)S(1)} %convolution_add_fusion.1, bf16[4096,1024]{1,0:T(8,128)(2,1)} %param.15, bf16[128,2048]{1,0:T(8,128)(2,1)S(1)} %copy-done.10), kind=kOutput, calls=%fused_computation.3 | convolution fusion | flops 1074790400 | bytes 11796480 | tf_op jit(solution)/shard_map/dot_general | solution.py:134
  285.4 5.8 %convolution_convert_fusion = bf16[128,4096]{1,0:T(8,128)(2,1)} fusion(bf16[128,1024]{0,1:T(8,128)(2,1)S(1)} %bitcast.81, bf16[1024,4096]{1,0:T(8,128)(2,1)} %param.16), kind=kOutput, calls=%fused_computation.4 | convolution fusion | flops 1074266112 | bytes 9699328 | tf_op jit(solution)/shard_map/dot_general | solution.py:85
  291.3 18.6 %reduce-scatter.8.cloned.1.call-done = bf16[128,1024]{1,0:T(8,128)(2,1)} async-done(((bf16[128,4096]{1,0:T(8,128)(2,1)}), bf16[128,1024]{1,0:T(8,128)(2,1)}) %reduce-scatter.8.cloned.1.call-update) | async-done | bytes 262160 | tf_op jit(solution)/shard_map/reduce_scatter | solution.py:136
  309.9 1.1 fusion.50
  311.0 5.8 %psum.7 = f32[128]{0:T(128)S(1)} all-reduce(f32[128]{0:T(128)S(1)} %fusion.50), channel_id=1, replica_groups=mesh['seq'=8,'tp'=4] {'tp'}, use_global_device_ids=true, to_apply=%region_11.12 | all-reduce | flops 128 | bytes 1024 | tf_op jit(solution)/shard_map/psum | solution.py:140
  316.8 20.5 %reduce-scatter.6.cloned.1.call-done = bf16[128,1024]{1,0:T(8,128)(2,1)} async-done(((bf16[128,4096]{1,0:T(8,128)(2,1)}), bf16[128,1024]{1,0:T(8,128)(2,1)}) %reduce-scatter.6.cloned.1.call-update) | async-done | bytes 262160 | tf_op jit(solution)/shard_map/reduce_scatter | solution.py:88
  337.3 2.2 fusion.45
  (48 shorter events, 1.1 us)
Async XLA Ops:
  7.2 20.4 %copy-start = (bf16[1280,1024]{1,0:T(8,128)(2,1)S(1)}, bf16[1280,1024]{1,0:T(8,128)(2,1)}, u32[]{:S(2)}) copy-start(bf16[1280,1024]{1,0:T(8,128)(2,1)} %param.11) | copy-start | bytes 7864324
  7.2 38.7 %all-gather.5.cloned.1.call-start = ((), (), s32[]{:S(2)}) async-start(), calls=%async_computation.3 | async-start | bytes 1310720 | tf_op jit(solution)/shard_map/all_gather | solution.py:44
  9.4 5.1 %collective-permute-start.1 = (f32[1]{0:T(128)}, f32[1]{0:T(128)}, u32[]{:S(2)}, u32[]{:S(2)}) collective-permute-start(f32[1]{0:T(128)} %bitcast.3), channel_id=1, source_target_pairs={{1,0},{2,1},{3,2},{4,3},{5,4},{6,5},{7,6},{8,7},{9,8},{10,9},{11,1... | collective-permute-start | bytes 20 | tf_op jit(solution)/shard_map/ppermute | solution.py:17
  12.0 16.9 %copy-start.11 = (s32[32,32]{1,0:T(8,128)S(1)}, s32[32,32]{1,0:T(8,128)}, u32[]{:S(2)}) copy-start(s32[32,32]{1,0:T(8,128)} %param.10) | copy-start | bytes 12292
  12.0 17.1 %copy-start.8 = (bf16[128,1024]{1,0:T(8,128)(2,1)S(1)}, bf16[128,1024]{1,0:T(8,128)(2,1)}, u32[]{:S(2)}) copy-start(bf16[128,1024]{1,0:T(8,128)(2,1)} %param.17) | copy-start | bytes 786436
  12.0 3.8 %collective-permute-start = (f32[1,1280]{1,0:T(1,128)S(1)}, f32[1,1280]{1,0:T(1,128)S(1)}, u32[]{:S(2)}, u32[]{:S(2)}) collective-permute-start(f32[1,1280]{1,0:T(1,128)S(1)} %fusion.71), channel_id=1, source_target_pairs={{1,0},{2,1},{3,2},{4,3},{5,4},{6,5},{7,6},{8,7},{9,8},{10,9},{11,1... | collective-permute-start | bytes 15368 | tf_op jit(solution)/shard_map/ppermute | solution.py:17
  27.6 19.8 %copy-start.9 = (f32[4096]{0:T(1024)S(1)}, f32[4096]{0:T(1024)}, u32[]{:S(2)}) copy-start(f32[4096]{0:T(1024)} %param.12) | copy-start | bytes 49156
  28.8 35.4 %all-gather.11.cloned.1.call-start = ((), (), s32[]{:S(2)}) async-start(), calls=%async_computation.7 | async-start | bytes 1310720 | tf_op jit(solution)/shard_map/all_gather | solution.py:95
  29.9 86.1 %all-gather.9.cloned.1.call-start = ((), (), s32[]{:S(2)}) async-start(), calls=%async_computation.5 | async-start | bytes 2359296 | tf_op jit(solution)/shard_map/all_gather | solution.py:60
  47.4 5.8 %copy-start.2 = (bf16[128,4096]{1,0:T(8,128)(2,1)S(1)}, bf16[128,4096]{1,0:T(8,128)(2,1)}, u32[]{:S(2)}) copy-start(bf16[128,4096]{1,0:T(8,128)(2,1)} %all-gather.5.cloned.1.call-done) | copy-start | bytes 3145732
  53.2 112.5 %all-gather.7.cloned.1.call-start = ((), (), s32[]{:S(2)}) async-start(), calls=%async_computation.4 | async-start | bytes 2359296 | tf_op jit(solution)/shard_map/all_gather | solution.py:61
  58.9 211.6 %reduce-scatter.10.cloned.1.call-start = ((), (), s32[]{:S(2)}) async-start(), calls=%async_computation.9 | async-start | bytes 4718592
  165.7 4.0 %copy-start.5 = (f32[8,128,1024]{2,1,0:T(8,128)S(1)}, f32[8,128,1024]{2,1,0:T(8,128)}, u32[]{:S(2)}) copy-start(f32[8,128,1024]{2,1,0:T(8,128)} %get-tuple-element.9) | copy-start | bytes 12582916
  165.7 4.7 %copy-start.6 = (bf16[1024,1024]{1,0:T(8,128)(2,1)S(1)}, bf16[1024,1024]{1,0:T(8,128)(2,1)}, u32[]{:S(2)}) copy-start(bf16[1024,1024]{1,0:T(8,128)(2,1)} %all-gather.7.cloned.1.call-done) | copy-start | bytes 6291460
  171.6 1.4 copy-start.3
  173.0 1.6 copy-start.7
  183.5 126.4 %reduce-scatter.8.cloned.1.call-start = ((), (), s32[]{:S(2)}) async-start(), calls=%async_computation.8 | async-start | bytes 1310720 | tf_op jit(solution)/shard_map/reduce_scatter | solution.py:136
  271.7 6.4 %copy-start.10 = (bf16[128,2048]{1,0:T(8,128)(2,1)S(1)}, bf16[128,2048]{1,0:T(8,128)(2,1)}, u32[]{:S(2)}) copy-start(bf16[128,2048]{1,0:T(8,128)(2,1)} %reduce-scatter.10.cloned.1.call-done) | copy-start | bytes 1572868
  285.3 51.9 %reduce-scatter.6.cloned.1.call-start = ((), (), s32[]{:S(2)}) async-start(), calls=%async_computation.6 | async-start | bytes 1310720 | tf_op jit(solution)/shard_map/reduce_scatter | solution.py:88
  285.4 24.5 %copy-start.4 = (bf16[128,1024]{1,0:T(8,128)(2,1)S(1)}, bf16[128,1024]{1,0:T(8,128)(2,1)}, u32[]{:S(2)}) copy-start(bf16[128,1024]{1,0:T(8,128)(2,1)} %convolution_convert_fusion.3) | copy-start | bytes 786436
  285.4 54.1 %copy-start.1 = (bf16[1280,1024]{1,0:T(8,128)(2,1)S(1)}, bf16[1280,1024]{1,0:T(8,128)(2,1)}, u32[]{:S(2)}) copy-start(bf16[1280,1024]{1,0:T(8,128)(2,1)} %param.11) | copy-start | bytes 7864324
Sparse Core Ops, SparseCore 0:
  28.9 16.8 all-gather.4
  47.4 16.6 all-gather.10
  66.9 49.1 all-gather.8
  118.0 47.5 all-gather.6
  183.6 86.8 reduce-scatter.9
  285.4 24.4 reduce-scatter.7
  312.4 24.7 reduce-scatter.5
where the time goes:
time: 347 us; the launch traced here: 346 us
  waiting for transfers between devices  217 us (63%)
  matrix products  69.3 us (20%)
  blocking collectives  16.1 us (5%)
  between operations  15 us (4%)
  local copies, waits for them, and re-layouts  14.1 us (4%)
  other arithmetic  11.3 us (3%)
    unnamed x8, waiting for transfers between devices  78.2 us
    all_gather x1, waiting for transfers between devices, per_device(): lax.all_gather(key_rows, 'seq', axis=0, tiled=True)  40.2 us
    all_gather x1, waiting for transfers between devices, per_device(): lax.all_gather(value_rows, 'seq', axis=0, tiled=True)  38.1 us
    reduce_scatter x1, waiting for transfers between devices, per_device(): lax.psum_scatter(partial_value.astype(jnp.bfloat16), 'tp', scatter_dimens...  20.5 us
    reduce_scatter x1, waiting for transfers between devices, per_device(): lax.psum_scatter(dnormed.astype(jnp.bfloat16), 'tp', scatter_dimension=1,...  18.6 us
    all_gather x1, waiting for transfers between devices, per_device(): lax.all_gather(latent_in, 'tp', axis=1, tiled=True).astype(jnp.float32)  15.9 us
    all_gather x1, blocking collectives, per_device(): group = lax.all_gather(patches, 'tp', axis=0, tiled=True)  10.4 us
    unnamed x26, local copies, waits for them, and re-layouts  9.65 us
  transfers between devices with their start and end apart: 9, of which 8 were waited for; matrix products, arithmetic and copies ran while one was open for 16% of the time, Pallas kernels for 0%

commit v1 on v0

--- a/solution.py
+++ b/solution.py
@@ -1,6 +1,10 @@
+import functools
+
 import jax
 import jax.numpy as jnp
 from jax import lax
+from jax.experimental import pallas as pl
+from jax.experimental.pallas import tpu as pltpu
 from jax.sharding import PartitionSpec as P
 
 HEAD_DIM = 128
@@ -146,6 +150,242 @@
     return (latent_out, latent_grad)
 
 
+MESH = pl.DeviceIdType.MESH
+
+
+def block(ref, dim, index, size):
+    at = pl.ds(pl.multiple_of(index * size, size), size)
+    return ref.at[at, :] if dim == 0 else ref.at[:, at]
+
+
+def greet(axis, me, n):
+    barrier = pltpu.get_barrier_semaphore()
+    for offset in range(1, n):
+        pl.semaphore_signal(
+            barrier, inc=1, device_id={axis: lax.rem(me + offset, n)}, device_id_type=MESH
+        )
+    pl.semaphore_wait(barrier, n - 1)
+
+
+def swap_kernel(axis, n, count, src_dim, dst_dim, *refs):
+    sources, targets = refs[:count], refs[count : 2 * count]
+    send_sem, recv_sem, own_sem = refs[2 * count :]
+    me = lax.axis_index(axis)
+    greet(axis, me, n)
+    copies = []
+    for i in range(count):
+        src_size = sources[i].shape[src_dim] // n
+        dst_size = targets[i].shape[dst_dim] // n
+        landing = block(targets[i], dst_dim, me, dst_size)
+        for offset in range(1, n):
+            peer = lax.rem(me + offset, n)
+            copy = pltpu.make_async_remote_copy(
+                src_ref=block(sources[i], src_dim, peer, src_size),
+                dst_ref=landing,
+                send_sem=send_sem.at[i, offset],
+                recv_sem=recv_sem.at[i, offset],
+                device_id={axis: peer},
+                device_id_type=MESH,
+            )
+            copy.start()
+            copies.append(copy)
+        own = pltpu.make_async_copy(
+            block(sources[i], src_dim, me, src_size), landing, own_sem.at[i]
+        )
+        own.start()
+        copies.append(own)
+    for copy in copies:
+        copy.wait()
+
+
+def swap(arrays, axis, src_dim, dst_dim, collective_id):
+    n, count = lax.axis_size(axis), len(arrays)
+    shapes = []
+    for array in arrays:
+        shape = list(array.shape)
+        shape[src_dim] //= n
+        shape[dst_dim] *= n
+        shapes.append(jax.ShapeDtypeStruct(tuple(shape), array.dtype))
+    return pl.pallas_call(
+        functools.partial(swap_kernel, axis, n, count, src_dim, dst_dim),
+        out_shape=shapes,
+        in_specs=[pl.BlockSpec(memory_space=pltpu.VMEM)] * count,
+        out_specs=[pl.BlockSpec(memory_space=pltpu.VMEM)] * count,
+        scratch_shapes=[
+            pltpu.SemaphoreType.DMA((count, n)),
+            pltpu.SemaphoreType.DMA((count, n)),
+            pltpu.SemaphoreType.DMA((count,)),
+        ],
+        compiler_params=pltpu.CompilerParams(
+            collective_id=collective_id, has_side_effects=True
+        ),
+    )(*arrays)
+
+
+def collect_kernel(axis, n, count, dim, *refs):
+    sources, targets = refs[:count], refs[count : 2 * count]
+    send_sem, recv_sem, own_sem = refs[2 * count :]
+    me = lax.axis_index(axis)
+    partner = me + 1 - 2 * lax.rem(me, 2)
+    half = n // 2
+    greet(axis, me, n)
+
+    def send(i, src, dst, slot, peer):
+        copy = pltpu.make_async_remote_copy(
+            src_ref=src,
+            dst_ref=dst,
+            send_sem=send_sem.at[i, slot],
+            recv_sem=recv_sem.at[i, slot],
+            device_id={axis: peer},
+            device_id_type=MESH,
+        )
+        copy.start()
+        return copy
+
+    far, near = [], []
+    for i in range(count):
+        size = sources[i].shape[dim]
+        for step in range(1, half):
+            peer = lax.rem(me + 2 * step, n)
+            landing = block(targets[i], dim, me, size)
+            far.append((i, step, send(i, sources[i], landing, step, peer)))
+    for i in range(count):
+        landing = block(targets[i], dim, me, sources[i].shape[dim])
+        near.append(send(i, sources[i], landing, 0, partner))
+        own = pltpu.make_async_copy(sources[i], landing, own_sem.at[i])
+        own.start()
+        near.append(own)
+    for i, step, copy in far:
+        copy.wait_recv()
+        origin = lax.rem(me + n - 2 * step, n)
+        arrived = block(targets[i], dim, origin, sources[i].shape[dim])
+        near.append(send(i, arrived, arrived, half + step, partner))
+    for _, _, copy in far:
+        copy.wait_send()
+    for copy in near:
+        copy.wait()
+
+
+def collect(arrays, axis, dim, collective_id):
+    n, count = lax.axis_size(axis), len(arrays)
+    shapes = []
+    for array in arrays:
+        shape = list(array.shape)
+        shape[dim] *= n
+        shapes.append(jax.ShapeDtypeStruct(tuple(shape), array.dtype))
+    return pl.pallas_call(
+        functools.partial(collect_kernel, axis, n, count, dim),
+        out_shape=shapes,
+        in_specs=[pl.BlockSpec(memory_space=pltpu.VMEM)] * count,
+        out_specs=[pl.BlockSpec(memory_space=pltpu.VMEM)] * count,
+        scratch_shapes=[
+            pltpu.SemaphoreType.DMA((count, n)),
+            pltpu.SemaphoreType.DMA((count, n)),
+            pltpu.SemaphoreType.DMA((count,)),
+        ],
+        compiler_params=pltpu.CompilerParams(
+            collective_id=collective_id, has_side_effects=True
+        ),
+    )(*arrays)
+
+
+def one_head(query, keys, values, d_attn, allowed):
+    scale = HEAD_DIM ** (-0.5)
+    scores = lax.dot_general(query, keys, CONTRACT_LAST, preferred_element_type=jnp.float32)
+    scores = scores * scale
+    peak = jnp.max(jnp.where(allowed, scores, NEG), 1)
+    expo = jnp.where(allowed, jnp.exp(scores - peak[:, None]), 0.0)
+    total = jnp.sum(expo, 1)
+    mixed = jnp.dot(expo.astype(jnp.bfloat16), values, preferred_element_type=jnp.float32)
+    attn = (mixed / total[:, None]).astype(jnp.bfloat16)
+    delta = jnp.sum(d_attn.astype(jnp.float32) * attn.astype(jnp.float32), 1)
+    probs = expo / total[:, None]
+    d_probs = lax.dot_general(d_attn, values, CONTRACT_LAST, preferred_element_type=jnp.float32)
+    d_scores = (probs * (d_probs - delta[:, None])).astype(jnp.bfloat16)
+    rows = (((0,), (0,)), ((), ()))
+    grad_query = jnp.dot(d_scores, keys, preferred_element_type=jnp.float32) * scale
+    grad_key = lax.dot_general(d_scores, query, rows, preferred_element_type=jnp.float32) * scale
+    grad_value = lax.dot_general(
+        probs.astype(jnp.bfloat16), d_attn, rows, preferred_element_type=jnp.float32
+    )
+    low = jnp.bfloat16
+    return attn, grad_query.astype(low), grad_key.astype(low), grad_value.astype(low)
+
+
+def per_device_heads(encoded, starts, w_up, norm_gain, w_query, w_key, w_value, w_out, cotangent):
+    byte_rows = encoded.shape[0]
+    patch_cap = starts.shape[1]
+    model_width = norm_gain.shape[0]
+    shard = lax.axis_index(("seq", "tp"))
+    own_starts = lax.dynamic_slice_in_dim(starts, shard, 1, 0)[0]
+    places = jnp.arange(byte_rows, dtype=jnp.int32)
+    following = jnp.concatenate([own_starts[1:], jnp.full((1,), byte_rows, jnp.int32)])
+    inside = (places[None, :] >= own_starts[:, None]) & (places[None, :] < following[:, None])
+    sums = jnp.dot(inside.astype(jnp.bfloat16), encoded, preferred_element_type=jnp.float32)
+    sizes = jnp.sum(inside.astype(jnp.float32), 1)
+    leading = places[None, :] < own_starts[:1, None]
+    lead_sum = jnp.dot(leading.astype(jnp.bfloat16), encoded, preferred_element_type=jnp.float32)
+    lead_size = jnp.sum(leading.astype(jnp.float32), 1)
+    next_sum, next_size = shifted((lead_sum, lead_size), ("seq", "tp"), -1)
+    count = jnp.sum((own_starts < byte_rows).astype(jnp.int32))
+    last_slot = (jnp.arange(patch_cap, dtype=jnp.int32) == count - 1).astype(jnp.float32)
+    sums = sums + last_slot[:, None] * next_sum
+    sizes = sizes + last_slot * next_size
+    patches = (sums / jnp.maximum(sizes, 1.0)[:, None]).astype(jnp.bfloat16)
+    (group,) = collect([patches], "tp", 0, 0)
+    latent_in = jnp.dot(group, w_up, preferred_element_type=jnp.float32).astype(jnp.bfloat16)
+    group_rows, columns = latent_in.shape
+    valid_all = (starts < byte_rows).reshape(starts.size)
+    row_base = lax.axis_index("seq") * group_rows
+    query_valid = lax.dynamic_slice_in_dim(valid_all, row_base, group_rows, 0)
+    grad_out = jnp.where(query_valid[:, None], cotangent, jnp.zeros_like(cotangent))
+    wide_low, wide_grad = collect([latent_in, grad_out], "tp", 1, 1)
+    wide_piece = wide_low.astype(jnp.float32)
+    scaled = (wide_piece * norm_gain[None, :]).astype(jnp.bfloat16)
+    rinv = lax.rsqrt(jnp.sum(wide_piece * wide_piece, 1) / model_width + EPS)
+
+    def project(weight):
+        acc = jnp.dot(scaled, weight, preferred_element_type=jnp.float32)
+        return (rinv[:, None] * acc).astype(jnp.bfloat16)
+
+    d_attn_rows = lax.dot_general(
+        wide_grad, w_out, CONTRACT_LAST, preferred_element_type=jnp.float32
+    ).astype(jnp.bfloat16)
+    query, keys, values, d_attn = swap(
+        [project(w_query), project(w_key), project(w_value), d_attn_rows], "seq", 1, 0, 2
+    )
+    index = jnp.arange(starts.size, dtype=jnp.int32)
+    allowed = valid_all[None, :] & (index[None, :] <= index[:, None])
+    pieces = []
+    for start in range(0, query.shape[1], HEAD_DIM):
+        cut = slice(start, start + HEAD_DIM)
+        pieces.append(one_head(query[:, cut], keys[:, cut], values[:, cut], d_attn[:, cut], allowed))
+    joined = [p[0] if len(p) == 1 else jnp.concatenate(p, 1) for p in zip(*pieces)]
+    attn, grad_query, grad_key, grad_value = swap(joined, "seq", 0, 1, 3)
+    partial_value = jnp.dot(attn, w_out, preferred_element_type=jnp.float32).astype(jnp.bfloat16)
+    dnormed = (
+        lax.dot_general(grad_query, w_query, CONTRACT_LAST, preferred_element_type=jnp.float32)
+        + lax.dot_general(grad_key, w_key, CONTRACT_LAST, preferred_element_type=jnp.float32)
+        + lax.dot_general(grad_value, w_value, CONTRACT_LAST, preferred_element_type=jnp.float32)
+    ).astype(jnp.bfloat16)
+    value_parts, grad_parts = swap([partial_value, dnormed], "tp", 1, 0, 4)
+
+    def add_up(parts):
+        return jnp.sum(parts.reshape(-1, group_rows, columns).astype(jnp.float32), 0)
+
+    wide_in = latent_in.astype(jnp.float32)
+    latent_out = jnp.where(query_valid[:, None], wide_in + add_up(value_parts), 0.0)
+    normed_grad = add_up(grad_parts)
+    gain_own = lax.dynamic_slice_in_dim(norm_gain, lax.axis_index("tp") * columns, columns, 0)
+    dots = lax.psum(jnp.sum(gain_own[None, :] * normed_grad * wide_in, 1), "tp")
+    latent_grad = (
+        grad_out.astype(jnp.float32)
+        + rinv[:, None] * gain_own[None, :] * normed_grad
+        - wide_in * (rinv**3)[:, None] * dots[:, None] / model_width
+    )
+    return (latent_out.astype(jnp.bfloat16), latent_grad)
+
+
 def solution(mesh):
     in_specs = (
         P(("seq", "tp"), None),
@@ -159,6 +399,12 @@
         P("seq", "tp"),
     )
     out_specs = (P("seq", "tp"), P("seq", "tp"))
+
+    def choose(*arrays):
+        heads = arrays[4].shape[1] // HEAD_DIM
+        whole_heads = heads % lax.axis_size("seq") == 0 and lax.axis_size("tp") % 2 == 0
+        return (per_device_heads if whole_heads else per_device)(*arrays)
+
     return jax.shard_map(
-        per_device, mesh=mesh, in_specs=in_specs, out_specs=out_specs, check_vma=False
-    )
+        choose, mesh=mesh, in_specs=in_specs, out_specs=out_specs, check_vma=False
+    )

time: 347 us -> 197 us (0.57)
  waiting for transfers between devices: 217 us -> 0.01 us
  Pallas kernels: 0 us -> 115 us
  matrix products: 69.3 us -> 53 us
  between operations: 15 us -> 1.67 us
  local copies, waits for them, and re-layouts: 14.1 us -> 2.2 us
  blocking collectives: 16.1 us -> 7.55 us
    pallas_call x0 -> x5, Pallas kernels: none -> 115 us  [the longest x3 87.2 us: swap(): pl.pallas_call(functools.partial(swap_kernel, axis, n, count, src_dim, ds...]
    all_gather x4 -> x0, waiting for transfers between devices: 99.1 us -> none  [the longest x1 40.2 us: per_device(): lax.all_gather(key_rows, 'seq', axis=0, tiled=True)]
    unnamed x8 -> x0, waiting for transfers between devices: 78.2 us -> none
    reduce_scatter x2 -> x0, waiting for transfers between devices: 39.1 us -> none  [the longest x1 20.5 us: per_device(): lax.psum_scatter(partial_value.astype(jnp.bfloat16), 'tp', scatter_dimens...]
    dot_general x16 -> x17, matrix products: 65 us -> 53 us  [the longest x3 9.81 us: project(): acc = jnp.dot(scaled, weight, preferred_element_type=jnp.float32)]
    all_gather x1 -> x0, blocking collectives: 10.4 us -> none  [per_device(): group = lax.all_gather(patches, 'tp', axis=0, tiled=True)]
    unnamed x26 -> x40, local copies, waits for them, and re-layouts: 9.65 us -> 1.27 us
    sub x1 -> x0, matrix products: 4.23 us -> none  [per_device(): expo = jnp.where(allowed[None], jnp.exp(scores - peak[:, :, None]), 0.0)]
  transfers between devices with their start and end apart: 9 -> 2, of which waited for: 8 -> 0; matrix products, arithmetic and copies ran while one was open for 16% -> 3% of each run, Pallas kernels for 0% -> 0%
where the time goes in v1:
time: 197 us
  Pallas kernels  115 us (58%)
  matrix products  53 us (27%)
  other arithmetic  14.4 us (7%)
  blocking collectives  7.55 us (4%)
  starting transfers between devices  2.58 us (1%)
  local copies, waits for them, and re-layouts  2.2 us (1%)
    pallas_call x3, Pallas kernels, swap(): pl.pallas_call(functools.partial(swap_kernel, axis, n, count, src_dim, ds...  87.2 us
    pallas_call x2, Pallas kernels, collect(): pl.pallas_call(functools.partial(collect_kernel, axis, n, count, dim), ou...  28 us
    dot_general x3, matrix products, project(): acc = jnp.dot(scaled, weight, preferred_element_type=jnp.float32)  9.81 us
    psum x1, blocking collectives, per_device_heads(): dots = lax.psum(jnp.sum(gain_own[None, :] * normed_grad * wide_in, 1), 'tp')  7.55 us
    dot_general x1, matrix products, per_device_heads(): lax.dot_general(grad_key, w_key, CONTRACT_LAST, preferred_element_type=jn...  6.42 us
    dot_general x1, matrix products, per_device_heads(): lax.dot_general(grad_query, w_query, CONTRACT_LAST, preferred_element_typ...  6.38 us
    dot_general x1, matrix products, per_device_heads(): jnp.dot(attn, w_out, preferred_element_type=jnp.float32)  5.76 us
  transfers between devices with their start and end apart: 2, of which 0 were waited for; matrix products, arithmetic and copies ran while one was open for 3% of the time, Pallas kernels for 0%

profile of v1, /device:TPU:0, one launch (start us, length us, event | category | flops | bytes accessed | tf_op | source)
XLA Modules:
  0.0 196.5 jit_solution(8077612442410196391)
XLA Ops:
  0.6 0.0 copy-start
  0.7 1.5 fusion.41
  2.1 0.7 fusion.38
  2.8 1.3 collective-permute-start.1
  4.2 1.3 fusion.43
  5.5 1.3 collective-permute-start
  6.8 0.1 slice_bitcast_fusion
  6.8 0.7 broadcast_compare_fusion
  8.2 0.1 reshape.65
  8.3 0.1 pad_add_fusion
  8.4 0.2 convert_reduce_fusion.2
  8.6 0.1 dynamic_slice.9
  8.6 1.7 broadcast_select_fusion.refs_1_
  10.4 0.7 dynamic_slice.11
  11.1 0.6 fusion.40
  11.7 2.0 %divide_convert_fusion.refs_0_ = bf16[32,1280]{1,0:T(8,128)(2,1)} fusion(f32[32]{0:T(128)S(1)} %fusion.40, f32[1280]{0:T(1024)S(1)} %reduce.1, f32[32]{0:T(128)S(1)} %compare_convert_fusion.2, bf16[256,1280]{1,0:T(8,128)(2,1)} %param.9, s32[32]{0:T(128)S(1)} %pad_add_fusion, s32[32]{0:T(128)S(1)} %bitcast.53), kind=kOutput, calls=%fused_computation.46 | convolution fusion | flops 21159936 | bytes 742912 | tf_op jit(solution)/shard_map/dot_general | solution.py:324
  13.7 9.9 %shard_map.104 = bf16[128,1280]{1,0:T(8,128)(2,1)} custom-call(bf16[32,1280]{1,0:T(8,128)(2,1)} %divide_convert_fusion.refs_0_), custom_call_target="tpu_custom_call" | custom-call | tf_op jit(solution)/shard_map/pallas_call | solution.py:276
  23.7 2.2 %convolution_convert_fusion.2.refs_0_ = bf16[128,1024]{1,0:T(8,128)(2,1)} fusion(bf16[128,1280]{1,0:T(8,128)(2,1)} %shard_map.104, bf16[1280,1024]{1,0:T(8,128)(2,1)S(1)} %copy-done), kind=kOutput, calls=%fused_computation.34 | convolution fusion | flops 335675392 | bytes 3211264 | tf_op jit(solution)/shard_map/dot_general | solution.py:336
  25.9 18.0 %shard_map.105 = (bf16[128,4096]{1,0:T(8,128)(2,1)}, bf16[128,4096]{1,0:T(8,128)(2,1)}) custom-call(bf16[128,1024]{1,0:T(8,128)(2,1)} %convolution_convert_fusion.2.refs_0_, bf16[128,1024]{1,0:T(8,128)(2,1)} %broadcast_select_fusion.refs_1_), custom_call_target="tpu_custom_call" | custom-call | tf_op jit(solution)/shard_map/pallas_call | solution.py:276
  43.9 1.7 fusion.2
  45.6 0.0 slice-start.1
  45.7 5.8 %fusion.14.refs_0_ = bf16[128,1024]{1,0:T(8,128)(2,1)} fusion(bf16[4096,1024]{1,0:T(8,128)(2,1)} %param.13, bf16[128,4096]{1,0:T(8,128)(2,1)} %get-tuple-element.14, f32[4096]{0:T(1024)S(1)} %copy-done.4, f32[128]{0:T(128)S(1)} %get-tuple-element.31), kind=kOutput, calls=%fused_computation.27 | convolution fusion | flops 1075576832 | bytes 9716224 | tf_op jit(solution)/shard_map/dot_general | solution.py:348
  51.5 0.0 slice-start.3
  51.5 2.0 %fusion.15.refs_1_ = bf16[128,1024]{1,0:T(8,128)(2,1)} fusion(bf16[4096,1024]{1,0:T(8,128)(2,1)S(1)} %bitcast.41, bf16[128,4096]{1,0:T(8,128)(2,1)S(1)} %copy-done.1, f32[4096]{0:T(1024)S(1)} %copy-done.4, f32[128]{0:T(128)S(1)} %get-tuple-element.31), kind=kOutput, calls=%fused_computation.28 | convolution fusion | flops 1075576832 | bytes 9716224 | tf_op jit(solution)/shard_map/dot_general | solution.py:348
  53.5 0.4 slice-done.3
  53.9 2.0 %fusion.16.refs_2_ = bf16[128,1024]{1,0:T(8,128)(2,1)} fusion(bf16[4096,1024]{1,0:T(8,128)(2,1)S(1)} %bitcast.43, bf16[128,4096]{1,0:T(8,128)(2,1)S(1)} %copy-done.1, f32[4096]{0:T(1024)S(1)} %copy-done.4, f32[128]{0:T(128)S(1)} %get-tuple-element.31), kind=kOutput, calls=%fused_computation.29 | convolution fusion | flops 1075576832 | bytes 9716224 | tf_op jit(solution)/shard_map/dot_general | solution.py:348
  55.9 0.5 slice-done.7
  56.4 0.3 copy-done.3
  56.7 3.6 %convolution_convert_fusion.1.refs_3_ = bf16[128,1024]{1,0:T(8,128)(2,1)} fusion(bf16[128,4096]{1,0:T(8,128)(2,1)S(1)} %copy-done.3, bf16[1024,4096]{1,0:T(8,128)(2,1)S(1)} %bitcast.47), kind=kOutput, calls=%fused_computation.30 | convolution fusion | flops 1073872896 | bytes 9699328 | tf_op jit(solution)/shard_map/dot_general | solution.py:351
  60.3 31.6 %shard_map.106 = (bf16[1024,128]{1,0:T(8,128)(2,1)}, bf16[1024,128]{1,0:T(8,128)(2,1)}, bf16[1024,128]{1,0:T(8,128)(2,1)}, bf16[1024,128]{1,0:T(8,128)(2,1)}) custom-call(bf16[128,1024]{1,0:T(8,128)(2,1)} %fusion.14.refs_0_, bf16[128,1024]{1,0:T(8,128)(2,1)} %fusion.15.refs_1_, bf16[128,1024]{1,0:T(8,128)(2,1)} %fusion.16.refs_2_, ...), custom_call_target="tpu_custom_call" | custom-call | tf_op jit(solution)/shard_map/pallas_call | solution.py:209
  91.9 1.8 select_reduce_fusion
  93.8 1.9 fusion.42
  95.8 1.7 multiply_reduce_fusion
  97.5 2.5 %multiply_convert_fusion = bf16[1024,1024]{0,1:T(8,128)(2,1)S(1)} fusion(bf16[1024,128]{1,0:T(8,128)(2,1)S(1)} %copy-done.8, bf16[1024,128]{1,0:T(8,128)(2,1)S(1)} %copy-done.11, f32[1024]{0:T(1024)S(1)} %get-tuple-element.34, f32[1024]{0:T(1024)S(1)} %fusion.42, f32[1024]{0:T(1024)S(1)} %get-tuple-element.32, f32[1024,1024]{0,1:T(8,128)S(1)} %get-tuple-element.33, ...), kind=kOutput, calls=%fused_computation.4 | convolution fusion | flops 277872640 | bytes 6829056 | tf_op jit(solution)/shard_map/dot_general | solution.py:303
  100.0 1.5 fusion.17.refs_1_
  101.5 1.4 fusion.18.refs_2_
  102.9 2.8 %fusion.11.refs_3_ = bf16[1024,128]{1,0:T(8,128)(2,1)} fusion(bf16[1024,128]{1,0:T(8,128)(2,1)S(1)} %copy-done.8, f32[1024]{0:T(1024)S(1)} %fusion.42, f32[1024,1024]{0,1:T(8,128)S(1)} %get-tuple-element.33, f32[1024]{0:T(1024)S(1)} %get-tuple-element.32, pred[1024]{0:T(1024)(128)(4,1)S(1)} %reshape.65), kind=kOutput, calls=%fused_computation.26 | convolution fusion | flops 275906560 | bytes 4727808 | tf_op jit(solution)/shard_map/dot_general | solution.py:308
  105.7 29.1 %shard_map.107 = (bf16[128,1024]{1,0:T(8,128)(2,1)}, bf16[128,1024]{1,0:T(8,128)(2,1)}, bf16[128,1024]{1,0:T(8,128)(2,1)}, bf16[128,1024]{1,0:T(8,128)(2,1)}) custom-call(bf16[1024,128]{1,0:T(8,128)(2,1)} %get-tuple-element.35.refs_0_, bf16[1024,128]{1,0:T(8,128)(2,1)} %fusion.17.refs_1_, bf16[1024,128]{1,0:T(8,128)(2,1)} %fusion.18.refs_2_, ...), custom_call_target="tpu_custom_call" | custom-call | tf_op jit(solution)/shard_map/pallas_call | solution.py:209
  134.8 5.8 %convolution_convert_fusion.refs_0_ = bf16[128,4096]{1,0:T(8,128)(2,1)} fusion(bf16[128,1024]{1,0:T(8,128)(2,1)} %get-tuple-element.20, bf16[1024,4096]{1,0:T(8,128)(2,1)} %param.16), kind=kOutput, calls=%fused_computation.3 | convolution fusion | flops 1074266112 | bytes 9699328 | tf_op jit(solution)/shard_map/dot_general | solution.py:365
  140.6 6.4 %fusion.44 = f32[128,4096]{1,0:T(8,128)S(1)} fusion(bf16[128,1024]{1,0:T(8,128)(2,1)S(1)} %copy-done.7, bf16[4096,1024]{1,0:T(8,128)(2,1)} %param.13), kind=kOutput, calls=%fused_computation.71 | convolution fusion | flops 1073741824 | bytes 10747904 | tf_op jit(solution)/shard_map/dot_general | solution.py:367
  147.0 6.4 %convolution_add_fusion.1 = f32[128,4096]{1,0:T(8,128)S(1)} fusion(f32[128,4096]{1,0:T(8,128)S(1)} %fusion.44, bf16[128,1024]{1,0:T(8,128)(2,1)S(1)} %copy-done.6, bf16[4096,1024]{1,0:T(8,128)(2,1)} %param.14), kind=kOutput, calls=%fused_computation.1 | convolution fusion | flops 1074266112 | bytes 12845056 | tf_op jit(solution)/shard_map/dot_general | solution.py:368
  153.5 3.9 %fusion.refs_1_ = bf16[128,4096]{1,0:T(8,128)(2,1)} fusion(f32[128,4096]{1,0:T(8,128)S(1)} %convolution_add_fusion.1, bf16[128,1024]{1,0:T(8,128)(2,1)S(1)} %copy-done.5, bf16[4096,1024]{1,0:T(8,128)(2,1)S(1)} %bitcast.45), kind=kOutput, calls=%fused_computation.2 | convolution fusion | flops 1074790400 | bytes 11796480 | tf_op jit(solution)/shard_map/dot_general | solution.py:369
  157.3 26.4 %shard_map.108 = (bf16[512,1024]{1,0:T(8,128)(2,1)}, bf16[512,1024]{1,0:T(8,128)(2,1)}) custom-call(bf16[128,4096]{1,0:T(8,128)(2,1)} %convolution_convert_fusion.refs_0_, bf16[128,4096]{1,0:T(8,128)(2,1)} %fusion.refs_1_), custom_call_target="tpu_custom_call" | custom-call | tf_op jit(solution)/shard_map/pallas_call | solution.py:209
  183.8 1.5 convert_reduce_fusion
  185.2 0.2 fusion.30
  185.4 7.6 %psum.7 = f32[128]{0:T(128)S(1)} all-reduce(f32[128]{0:T(128)S(1)} %fusion.30), channel_id=1, replica_groups=mesh['seq'=8,'tp'=4] {'tp'}, use_global_device_ids=true, to_apply=%region_10.11 | all-reduce | flops 128 | bytes 1024 | tf_op jit(solution)/shard_map/psum | solution.py:380
  192.9 1.5 convert_reduce_fusion.1
  194.4 2.1 %fusion.29 = (f32[128,1024]{1,0:T(8,128)}, bf16[128,1024]{1,0:T(8,128)(2,1)}) fusion(bf16[128,1024]{1,0:T(8,128)(2,1)S(1)} %copy-done.2, f32[128,1024]{1,0:T(8,128)S(1)} %convert_reduce_fusion, f32[128]{0:T(128)S(1)} %psum.7, f32[128]{0:T(128)S(1)} %get-tuple-element.30, f32[1024]{0:T(1024)S(1)} %dynamic_slice.11, f32[128]{0:T(128)S(1)} %get-tuple-element.31, ...), kind=kLoop, calls=%fused_computation.42 | loop fusion | flops 1703936 | bytes 2365056 | tf_op jit(solution)/shard_map/sub | solution.py:382
  (45 shorter events, 0.2 us)
Async XLA Ops:
  0.6 23.1 %copy-start = (bf16[1280,1024]{1,0:T(8,128)(2,1)S(1)}, bf16[1280,1024]{1,0:T(8,128)(2,1)}, u32[]{:S(2)}) copy-start(bf16[1280,1024]{1,0:T(8,128)(2,1)} %param.11) | copy-start | bytes 7864324
  0.6 45.0 %copy-start.4 = (f32[4096]{0:T(1024)S(1)}, f32[4096]{0:T(1024)}, u32[]{:S(2)}) copy-start(f32[4096]{0:T(1024)} %param.12) | copy-start | bytes 49156
  2.8 8.3 %collective-permute-start.1 = (f32[1]{0:T(128)}, f32[1]{0:T(128)}, u32[]{:S(2)}, u32[]{:S(2)}) collective-permute-start(f32[1]{0:T(128)} %bitcast.3), channel_id=1, source_target_pairs={{1,0},{2,1},{3,2},{4,3},{5,4},{6,5},{7,6},{8,7},{9,8},{10,9},{11,1... | collective-permute-start | bytes 20 | tf_op jit(solution)/shard_map/ppermute | solution.py:21
  5.5 6.3 %collective-permute-start = (f32[1,1280]{1,0:T(1,128)S(1)}, f32[1,1280]{1,0:T(1,128)S(1)}, u32[]{:S(2)}, u32[]{:S(2)}) collective-permute-start(f32[1,1280]{1,0:T(1,128)S(1)} %fusion.43), channel_id=1, source_target_pairs={{1,0},{2,1},{3,2},{4,3},{5,4},{6,5},{7,6},{8,7},{9,8},{10,9},{11,1... | collective-permute-start | bytes 15368 | tf_op jit(solution)/shard_map/ppermute | solution.py:21
  43.9 7.5 %slice-start = ((s8[8388608]{0:T(1024)(128)(4,1)}), s8[4194304]{0:T(1024)(128)(4,1)S(1)}, s32[]{:S(2)}) async-start(s8[8388608]{0:T(1024)(128)(4,1)} %bitcast.40), calls=%async_computation | async-start | bytes 8388608
  45.6 5.9 %slice-start.1 = ((s8[8388608]{0:T(1024)(128)(4,1)}), s8[4194304]{0:T(1024)(128)(4,1)S(1)}, s32[]{:S(2)}) async-start(s8[8388608]{0:T(1024)(128)(4,1)} %bitcast.40), calls=%async_computation.1 | async-start | bytes 8388608
  45.6 5.8 %copy-start.1 = (bf16[128,4096]{1,0:T(8,128)(2,1)S(1)}, bf16[128,4096]{1,0:T(8,128)(2,1)}, u32[]{:S(2)}) copy-start(bf16[128,4096]{1,0:T(8,128)(2,1)} %get-tuple-element.14) | copy-start | bytes 3145732
  45.6 7.9 %slice-start.2 = ((s8[8388608]{0:T(1024)(128)(4,1)}), s8[4194304]{0:T(1024)(128)(4,1)S(1)}, s32[]{:S(2)}) async-start(s8[8388608]{0:T(1024)(128)(4,1)} %bitcast.42), calls=%async_computation.2 | async-start | bytes 8388608
  51.5 2.4 %slice-start.3 = ((s8[8388608]{0:T(1024)(128)(4,1)}), s8[4194304]{0:T(1024)(128)(4,1)S(1)}, s32[]{:S(2)}) async-start(s8[8388608]{0:T(1024)(128)(4,1)} %bitcast.42), calls=%async_computation.3 | async-start | bytes 8388608
  51.5 4.4 %slice-start.6 = ((s8[8388608]{0:T(1024)(128)(4,1)}), s8[4194304]{0:T(1024)(128)(4,1)S(1)}, s32[]{:S(2)}) async-start(s8[8388608]{0:T(1024)(128)(4,1)} %bitcast.46), calls=%async_computation.6 | async-start | bytes 8388608
  53.9 2.5 %slice-start.7 = ((s8[8388608]{0:T(1024)(128)(4,1)}), s8[4194304]{0:T(1024)(128)(4,1)S(1)}, s32[]{:S(2)}) async-start(s8[8388608]{0:T(1024)(128)(4,1)} %bitcast.46), calls=%async_computation.7 | async-start | bytes 8388608
  53.9 2.8 %copy-start.3 = (bf16[128,4096]{1,0:T(8,128)(2,1)S(1)}, bf16[128,4096]{1,0:T(8,128)(2,1)}, u32[]{:S(2)}) copy-start(bf16[128,4096]{1,0:T(8,128)(2,1)} %get-tuple-element.15) | copy-start | bytes 3145732
  91.9 3.8 %copy-start.8 = (bf16[1024,128]{1,0:T(8,128)(2,1)S(1)}, bf16[1024,128]{1,0:T(8,128)(2,1)}, u32[]{:S(2)}) copy-start(bf16[1024,128]{1,0:T(8,128)(2,1)} %get-tuple-element.19) | copy-start | bytes 786436
  91.9 3.8 %copy-start.11 = (bf16[1024,128]{1,0:T(8,128)(2,1)S(1)}, bf16[1024,128]{1,0:T(8,128)(2,1)}, u32[]{:S(2)}) copy-start(bf16[1024,128]{1,0:T(8,128)(2,1)} %get-tuple-element.18) | copy-start | bytes 786436
  97.5 2.5 %copy-start.10 = (bf16[1024,128]{1,0:T(8,128)(2,1)S(1)}, bf16[1024,128]{1,0:T(8,128)(2,1)}, u32[]{:S(2)}) copy-start(bf16[1024,128]{1,0:T(8,128)(2,1)} %get-tuple-element.17) | copy-start | bytes 786436
  100.0 1.5 copy-start.9
  134.8 5.8 %copy-start.7 = (bf16[128,1024]{1,0:T(8,128)(2,1)S(1)}, bf16[128,1024]{1,0:T(8,128)(2,1)}, u32[]{:S(2)}) copy-start(bf16[128,1024]{1,0:T(8,128)(2,1)} %get-tuple-element.21) | copy-start | bytes 786436
  140.5 6.4 %copy-start.6 = (bf16[128,1024]{1,0:T(8,128)(2,1)S(1)}, bf16[128,1024]{1,0:T(8,128)(2,1)}, u32[]{:S(2)}) copy-start(bf16[128,1024]{1,0:T(8,128)(2,1)} %get-tuple-element.22) | copy-start | bytes 786436
  140.6 12.9 %slice-start.4 = ((s8[8388608]{0:T(1024)(128)(4,1)}), s8[4194304]{0:T(1024)(128)(4,1)S(1)}, s32[]{:S(2)}) async-start(s8[8388608]{0:T(1024)(128)(4,1)} %bitcast.44), calls=%async_computation.4 | async-start | bytes 8388608
  147.0 6.5 %slice-start.5 = ((s8[8388608]{0:T(1024)(128)(4,1)}), s8[4194304]{0:T(1024)(128)(4,1)S(1)}, s32[]{:S(2)}) async-start(s8[8388608]{0:T(1024)(128)(4,1)} %bitcast.44), calls=%async_computation.5 | async-start | bytes 8388608
  147.0 6.5 %copy-start.5 = (bf16[128,1024]{1,0:T(8,128)(2,1)S(1)}, bf16[128,1024]{1,0:T(8,128)(2,1)}, u32[]{:S(2)}) copy-start(bf16[128,1024]{1,0:T(8,128)(2,1)} %get-tuple-element.23) | copy-start | bytes 786436
  153.4 31.8 %copy-start.2 = (bf16[128,1024]{1,0:T(8,128)(2,1)S(1)}, bf16[128,1024]{1,0:T(8,128)(2,1)}, u32[]{:S(2)}) copy-start(bf16[128,1024]{1,0:T(8,128)(2,1)} %convolution_convert_fusion.2.refs_0_) | copy-start | bytes 786436

commit v2 on v1

--- a/solution.py
+++ b/solution.py
@@ -368,7 +368,11 @@
         + lax.dot_general(grad_key, w_key, CONTRACT_LAST, preferred_element_type=jnp.float32)
         + lax.dot_general(grad_value, w_value, CONTRACT_LAST, preferred_element_type=jnp.float32)
     ).astype(jnp.bfloat16)
-    value_parts, grad_parts = swap([partial_value, dnormed], "tp", 1, 0, 4)
+    dot_parts = jnp.sum(norm_gain[None, :] * dnormed.astype(jnp.float32) * wide_piece, 1)
+    tp_size = lax.axis_size("tp")
+    dot_tile = jnp.broadcast_to(jnp.tile(dot_parts, tp_size)[None, :], (8, tp_size * group_rows))
+    value_parts, grad_parts, dot_rows = swap([partial_value, dnormed, dot_tile], "tp", 1, 0, 4)
+    dots = jnp.sum(dot_rows.reshape(tp_size, 8, group_rows)[:, 0], 0)
 
     def add_up(parts):
         return jnp.sum(parts.reshape(-1, group_rows, columns).astype(jnp.float32), 0)
@@ -377,7 +381,6 @@
     latent_out = jnp.where(query_valid[:, None], wide_in + add_up(value_parts), 0.0)
     normed_grad = add_up(grad_parts)
     gain_own = lax.dynamic_slice_in_dim(norm_gain, lax.axis_index("tp") * columns, columns, 0)
-    dots = lax.psum(jnp.sum(gain_own[None, :] * normed_grad * wide_in, 1), "tp")
     latent_grad = (
         grad_out.astype(jnp.float32)
         + rinv[:, None] * gain_own[None, :] * normed_grad

time: 197 us -> 191 us (0.970)
  blocking collectives: 7.55 us -> 0 us
  Pallas kernels: 115 us -> 117 us
    psum x1 -> x0, blocking collectives: 7.55 us -> none  [per_device_heads(): dots = lax.psum(jnp.sum(gain_own[None, :] * normed_grad * wide_in, 1), 'tp')]
    pallas_call x3, Pallas kernels: 87.2 us -> 89.5 us  [swap(): pl.pallas_call(functools.partial(swap_kernel, axis, n, count, src_dim, ds...]
where the time goes in v2:
time: 191 us; the launch traced here: 190 us
  Pallas kernels  117 us (61%)
  matrix products  53.3 us (28%)
  other arithmetic  13.2 us (7%)
  starting transfers between devices  2.58 us (1%)
  local copies, waits for them, and re-layouts  2.16 us (1%)
    pallas_call x3, Pallas kernels, swap(): pl.pallas_call(functools.partial(swap_kernel, axis, n, count, src_dim, ds...  89.5 us
    pallas_call x2, Pallas kernels, collect(): pl.pallas_call(functools.partial(collect_kernel, axis, n, count, dim), ou...  28 us
    dot_general x3, matrix products, project(): acc = jnp.dot(scaled, weight, preferred_element_type=jnp.float32)  9.79 us
    dot_general x1, matrix products, per_device_heads(): lax.dot_general(grad_key, w_key, CONTRACT_LAST, preferred_element_type=jn...  6.42 us
    dot_general x1, matrix products, per_device_heads(): lax.dot_general(grad_query, w_query, CONTRACT_LAST, preferred_element_typ...  6.38 us
    dot_general x1, matrix products, per_device_heads(): jnp.dot(attn, w_out, preferred_element_type=jnp.float32)  5.81 us
    dot_general x1, matrix products, per_device_heads(): lax.dot_general(grad_value, w_value, CONTRACT_LAST, preferred_element_typ...  4.03 us
  transfers between devices with their start and end apart: 2, of which 0 were waited for; matrix products, arithmetic and copies ran while one was open for 3% of the time, Pallas kernels for 0%

profile of v2, /device:TPU:0, one launch (start us, length us, event | category | flops | bytes accessed | tf_op | source)
XLA Modules:
  0.0 190.4 jit_solution(18104906805008592816)
XLA Ops:
  0.6 0.0 copy-start
  0.7 1.5 fusion.41
  2.1 0.7 fusion.38
  2.8 1.3 collective-permute-start.1
  4.2 1.3 fusion.43
  5.5 1.3 collective-permute-start
  6.8 0.1 slice_bitcast_fusion
  6.8 0.7 broadcast_compare_fusion
  8.2 0.1 reshape.70
  8.3 0.1 pad_add_fusion
  8.4 0.2 convert_reduce_fusion.2
  8.6 0.1 dynamic_slice.9
  8.7 1.7 broadcast_select_fusion.refs_1_
  10.4 0.6 fusion.40
  11.1 2.0 %divide_convert_fusion.refs_0_ = bf16[32,1280]{1,0:T(8,128)(2,1)} fusion(f32[32]{0:T(128)S(1)} %fusion.40, f32[1280]{0:T(1024)S(1)} %reduce.2, f32[32]{0:T(128)S(1)} %compare_convert_fusion.2, bf16[256,1280]{1,0:T(8,128)(2,1)} %param.9, s32[32]{0:T(128)S(1)} %pad_add_fusion, s32[32]{0:T(128)S(1)} %bitcast.56), kind=kOutput, calls=%fused_computation.46 | convolution fusion | flops 21159936 | bytes 742912 | tf_op jit(solution)/shard_map/dot_general | solution.py:324
  13.1 9.9 %shard_map.104 = bf16[128,1280]{1,0:T(8,128)(2,1)} custom-call(bf16[32,1280]{1,0:T(8,128)(2,1)} %divide_convert_fusion.refs_0_), custom_call_target="tpu_custom_call" | custom-call | tf_op jit(solution)/shard_map/pallas_call | solution.py:276
  23.1 2.2 %convolution_convert_fusion.2.refs_0_ = bf16[128,1024]{1,0:T(8,128)(2,1)} fusion(bf16[128,1280]{1,0:T(8,128)(2,1)} %shard_map.104, bf16[1280,1024]{1,0:T(8,128)(2,1)S(1)} %copy-done), kind=kOutput, calls=%fused_computation.36 | convolution fusion | flops 335675392 | bytes 3211264 | tf_op jit(solution)/shard_map/dot_general | solution.py:336
  25.2 18.0 %shard_map.105 = (bf16[128,4096]{1,0:T(8,128)(2,1)}, bf16[128,4096]{1,0:T(8,128)(2,1)}) custom-call(bf16[128,1024]{1,0:T(8,128)(2,1)} %convolution_convert_fusion.2.refs_0_, bf16[128,1024]{1,0:T(8,128)(2,1)} %broadcast_select_fusion.refs_1_), custom_call_target="tpu_custom_call" | custom-call | tf_op jit(solution)/shard_map/pallas_call | solution.py:276
  43.3 0.0 slice-start
  43.3 1.7 fusion.2
  45.0 0.0 slice-start.1
  45.0 5.8 %fusion.15.refs_0_ = bf16[128,1024]{1,0:T(8,128)(2,1)} fusion(bf16[4096,1024]{1,0:T(8,128)(2,1)} %param.13, bf16[128,4096]{1,0:T(8,128)(2,1)} %get-tuple-element.15, f32[4096]{0:T(1024)S(1)} %copy-done.4, f32[128]{0:T(128)S(1)} %get-tuple-element.33), kind=kOutput, calls=%fused_computation.29 | convolution fusion | flops 1075576832 | bytes 9716224 | tf_op jit(solution)/shard_map/dot_general | solution.py:348
  50.8 0.0 slice-start.3
  50.9 2.0 %fusion.16.refs_1_ = bf16[128,1024]{1,0:T(8,128)(2,1)} fusion(bf16[4096,1024]{1,0:T(8,128)(2,1)S(1)} %bitcast.44, bf16[128,4096]{1,0:T(8,128)(2,1)S(1)} %copy-done.1, f32[4096]{0:T(1024)S(1)} %copy-done.4, f32[128]{0:T(128)S(1)} %get-tuple-element.33), kind=kOutput, calls=%fused_computation.30 | convolution fusion | flops 1075576832 | bytes 9716224 | tf_op jit(solution)/shard_map/dot_general | solution.py:348
  52.9 0.4 slice-done.3
  53.2 2.0 %fusion.17.refs_2_ = bf16[128,1024]{1,0:T(8,128)(2,1)} fusion(bf16[4096,1024]{1,0:T(8,128)(2,1)S(1)} %bitcast.46, bf16[128,4096]{1,0:T(8,128)(2,1)S(1)} %copy-done.1, f32[4096]{0:T(1024)S(1)} %copy-done.4, f32[128]{0:T(128)S(1)} %get-tuple-element.33), kind=kOutput, calls=%fused_computation.31 | convolution fusion | flops 1075576832 | bytes 9716224 | tf_op jit(solution)/shard_map/dot_general | solution.py:348
  55.2 0.5 slice-done.7
  55.7 0.3 copy-done.5
  56.1 3.6 %convolution_convert_fusion.1.refs_3_ = bf16[128,1024]{1,0:T(8,128)(2,1)} fusion(bf16[128,4096]{1,0:T(8,128)(2,1)S(1)} %copy-done.5, bf16[1024,4096]{1,0:T(8,128)(2,1)S(1)} %bitcast.50), kind=kOutput, calls=%fused_computation.32 | convolution fusion | flops 1073872896 | bytes 9699328 | tf_op jit(solution)/shard_map/dot_general | solution.py:351
  59.6 31.7 %shard_map.106 = (bf16[1024,128]{1,0:T(8,128)(2,1)}, bf16[1024,128]{1,0:T(8,128)(2,1)}, bf16[1024,128]{1,0:T(8,128)(2,1)}, bf16[1024,128]{1,0:T(8,128)(2,1)}) custom-call(bf16[128,1024]{1,0:T(8,128)(2,1)} %fusion.15.refs_0_, bf16[128,1024]{1,0:T(8,128)(2,1)} %fusion.16.refs_1_, bf16[128,1024]{1,0:T(8,128)(2,1)} %fusion.17.refs_2_, ...), custom_call_target="tpu_custom_call" | custom-call | tf_op jit(solution)/shard_map/pallas_call | solution.py:209
  91.3 1.8 select_reduce_fusion
  93.2 2.0 %fusion.42 = f32[1024]{0:T(1024)S(1)} fusion(f32[1024]{0:T(1024)S(1)} %get-tuple-element.34, f32[1024,1024]{0,1:T(8,128)S(1)} %get-tuple-element.35, pred[1024]{0:T(1024)(128)(4,1)S(1)} %reshape.70), kind=kLoop, calls=%fused_computation.71 | loop fusion | flops 6290432 | bytes 4203520 | tf_op jit(solution)/shard_map/reduce_sum | solution.py:298
  95.2 1.7 multiply_reduce_fusion
  96.9 2.5 %multiply_convert_fusion = bf16[1024,1024]{0,1:T(8,128)(2,1)S(1)} fusion(bf16[1024,128]{1,0:T(8,128)(2,1)S(1)} %copy-done.10, bf16[1024,128]{1,0:T(8,128)(2,1)S(1)} %copy-done.13, f32[1024]{0:T(1024)S(1)} %get-tuple-element.36, f32[1024]{0:T(1024)S(1)} %fusion.42, f32[1024]{0:T(1024)S(1)} %get-tuple-element.34, f32[1024,1024]{0,1:T(8,128)S(1)} %get-tuple-element.35, ...), kind=kOutput, calls=%fused_computation.4 | convolution fusion | flops 277872640 | bytes 6829056 | tf_op jit(solution)/shard_map/dot_general | solution.py:303
  99.4 1.5 fusion.18.refs_1_
  100.9 1.4 fusion.19.refs_2_
  102.3 2.8 %fusion.12.refs_3_ = bf16[1024,128]{1,0:T(8,128)(2,1)} fusion(bf16[1024,128]{1,0:T(8,128)(2,1)S(1)} %copy-done.10, f32[1024]{0:T(1024)S(1)} %fusion.42, f32[1024,1024]{0,1:T(8,128)S(1)} %get-tuple-element.35, f32[1024]{0:T(1024)S(1)} %get-tuple-element.34, pred[1024]{0:T(1024)(128)(4,1)S(1)} %reshape.70), kind=kOutput, calls=%fused_computation.28 | convolution fusion | flops 275906560 | bytes 4727808 | tf_op jit(solution)/shard_map/dot_general | solution.py:308
  105.1 29.1 %shard_map.107 = (bf16[128,1024]{1,0:T(8,128)(2,1)}, bf16[128,1024]{1,0:T(8,128)(2,1)}, bf16[128,1024]{1,0:T(8,128)(2,1)}, bf16[128,1024]{1,0:T(8,128)(2,1)}) custom-call(bf16[1024,128]{1,0:T(8,128)(2,1)} %get-tuple-element.37.refs_0_, bf16[1024,128]{1,0:T(8,128)(2,1)} %fusion.18.refs_1_, bf16[1024,128]{1,0:T(8,128)(2,1)} %fusion.19.refs_2_, ...), custom_call_target="tpu_custom_call" | custom-call | tf_op jit(solution)/shard_map/pallas_call | solution.py:209
  134.2 5.8 %convolution_convert_fusion.refs_0_ = bf16[128,4096]{1,0:T(8,128)(2,1)} fusion(bf16[128,1024]{1,0:T(8,128)(2,1)} %get-tuple-element.21, bf16[1024,4096]{1,0:T(8,128)(2,1)} %param.16), kind=kOutput, calls=%fused_computation.3 | convolution fusion | flops 1074266112 | bytes 9699328 | tf_op jit(solution)/shard_map/dot_general | solution.py:365
  140.1 6.4 %fusion.44 = f32[128,4096]{1,0:T(8,128)S(1)} fusion(bf16[128,1024]{1,0:T(8,128)(2,1)S(1)} %copy-done.9, bf16[4096,1024]{1,0:T(8,128)(2,1)} %param.13), kind=kOutput, calls=%fused_computation.73 | convolution fusion | flops 1073741824 | bytes 10747904 | tf_op jit(solution)/shard_map/dot_general | solution.py:367
  146.5 0.0 slice-start.5
  146.5 6.4 %convolution_add_fusion.1 = f32[128,4096]{1,0:T(8,128)S(1)} fusion(f32[128,4096]{1,0:T(8,128)S(1)} %fusion.44, bf16[128,1024]{1,0:T(8,128)(2,1)S(1)} %copy-done.8, bf16[4096,1024]{1,0:T(8,128)(2,1)} %param.14), kind=kOutput, calls=%fused_computation.1 | convolution fusion | flops 1074266112 | bytes 12845056 | tf_op jit(solution)/shard_map/dot_general | solution.py:368
  153.0 4.0 %fusion.4 = (f32[128]{0:T(128)S(1)}, bf16[128,4096]{1,0:T(8,128)(2,1)}) fusion(bf16[128,4096]{1,0:T(8,128)(2,1)S(1)} %copy-done.2, f32[4096]{0:T(1024)S(1)} %copy-done.4, f32[128,4096]{1,0:T(8,128)S(1)} %convolution_add_fusion.1, bf16[128,1024]{1,0:T(8,128)(2,1)S(1)} %copy-done.7, bf16[4096,1024]{1,0:T(8,128)(2,1)S(1)} %bitcast.48), kind=kOutput, calls=%fused_computation.14 | convolution fusion | flops 1077411712 | bytes 12861952 | tf_op jit(solution)/shard_map/dot_general | solution.py:369
  157.0 0.6 broadcast_in_dim.32.refs_2_
  157.6 28.7 %shard_map.108 = (bf16[512,1024]{1,0:T(8,128)(2,1)}, bf16[512,1024]{1,0:T(8,128)(2,1)}, f32[32,128]{1,0:T(8,128)}) custom-call(bf16[128,4096]{1,0:T(8,128)(2,1)} %convolution_convert_fusion.refs_0_, bf16[128,4096]{1,0:T(8,128)(2,1)} %get-tuple-element.39.refs_1_, f32[8,512]{1,0:T(8,128)} %broadcast_in_dim.32.refs_2_), custom_call_target="tpu_custom_call" | custom-call | tf_op jit(solution)/shard_map/pallas_call | solution.py:209
  186.3 0.7 slice_reduce_fusion
  187.1 2.1 %convert_reduce_fusion = (f32[128,1024]{1,0:T(8,128)S(1)}, f32[128,1024]{1,0:T(8,128)S(1)}) fusion(bf16[4,128,1024]{2,1,0:T(8,128)(2,1)} %bitcast.52, bf16[4,128,1024]{2,1,0:T(8,128)(2,1)} %bitcast.51), kind=kLoop, calls=%fused_computation.15 | loop fusion | flops 1835008 | bytes 3145728 | tf_op jit(solution)/shard_map/reduce_sum | solution.py:378
  189.2 1.2 fusion.30
  (50 shorter events, 0.2 us)
Async XLA Ops:
  0.6 22.4 %copy-start = (bf16[1280,1024]{1,0:T(8,128)(2,1)S(1)}, bf16[1280,1024]{1,0:T(8,128)(2,1)}, u32[]{:S(2)}) copy-start(bf16[1280,1024]{1,0:T(8,128)(2,1)} %param.11) | copy-start | bytes 7864324
  0.6 44.3 %copy-start.4 = (f32[4096]{0:T(1024)S(1)}, f32[4096]{0:T(1024)}, u32[]{:S(2)}) copy-start(f32[4096]{0:T(1024)} %param.12) | copy-start | bytes 49156
  2.8 7.6 %collective-permute-start.1 = (f32[1]{0:T(128)}, f32[1]{0:T(128)}, u32[]{:S(2)}, u32[]{:S(2)}) collective-permute-start(f32[1]{0:T(128)} %bitcast.3), channel_id=1, source_target_pairs={{1,0},{2,1},{3,2},{4,3},{5,4},{6,5},{7,6},{8,7},{9,8},{10,9},{11,1... | collective-permute-start | bytes 20 | tf_op jit(solution)/shard_map/ppermute | solution.py:21
  5.5 5.6 %collective-permute-start = (f32[1,1280]{1,0:T(1,128)S(1)}, f32[1,1280]{1,0:T(1,128)S(1)}, u32[]{:S(2)}, u32[]{:S(2)}) collective-permute-start(f32[1,1280]{1,0:T(1,128)S(1)} %fusion.43), channel_id=1, source_target_pairs={{1,0},{2,1},{3,2},{4,3},{5,4},{6,5},{7,6},{8,7},{9,8},{10,9},{11,1... | collective-permute-start | bytes 15368 | tf_op jit(solution)/shard_map/ppermute | solution.py:21
  43.3 7.5 %slice-start = ((s8[8388608]{0:T(1024)(128)(4,1)}), s8[4194304]{0:T(1024)(128)(4,1)S(1)}, s32[]{:S(2)}) async-start(s8[8388608]{0:T(1024)(128)(4,1)} %bitcast.43), calls=%async_computation | async-start | bytes 8388608
  45.0 5.9 %slice-start.1 = ((s8[8388608]{0:T(1024)(128)(4,1)}), s8[4194304]{0:T(1024)(128)(4,1)S(1)}, s32[]{:S(2)}) async-start(s8[8388608]{0:T(1024)(128)(4,1)} %bitcast.43), calls=%async_computation.1 | async-start | bytes 8388608
  45.0 5.8 %copy-start.1 = (bf16[128,4096]{1,0:T(8,128)(2,1)S(1)}, bf16[128,4096]{1,0:T(8,128)(2,1)}, u32[]{:S(2)}) copy-start(bf16[128,4096]{1,0:T(8,128)(2,1)} %get-tuple-element.15) | copy-start | bytes 3145732
  45.0 7.9 %slice-start.2 = ((s8[8388608]{0:T(1024)(128)(4,1)}), s8[4194304]{0:T(1024)(128)(4,1)S(1)}, s32[]{:S(2)}) async-start(s8[8388608]{0:T(1024)(128)(4,1)} %bitcast.45), calls=%async_computation.2 | async-start | bytes 8388608
  50.8 2.4 %slice-start.3 = ((s8[8388608]{0:T(1024)(128)(4,1)}), s8[4194304]{0:T(1024)(128)(4,1)S(1)}, s32[]{:S(2)}) async-start(s8[8388608]{0:T(1024)(128)(4,1)} %bitcast.45), calls=%async_computation.3 | async-start | bytes 8388608
  50.9 4.4 %slice-start.6 = ((s8[8388608]{0:T(1024)(128)(4,1)}), s8[4194304]{0:T(1024)(128)(4,1)S(1)}, s32[]{:S(2)}) async-start(s8[8388608]{0:T(1024)(128)(4,1)} %bitcast.49), calls=%async_computation.6 | async-start | bytes 8388608
  53.2 2.5 %slice-start.7 = ((s8[8388608]{0:T(1024)(128)(4,1)}), s8[4194304]{0:T(1024)(128)(4,1)S(1)}, s32[]{:S(2)}) async-start(s8[8388608]{0:T(1024)(128)(4,1)} %bitcast.49), calls=%async_computation.7 | async-start | bytes 8388608
  53.2 2.8 %copy-start.5 = (bf16[128,4096]{1,0:T(8,128)(2,1)S(1)}, bf16[128,4096]{1,0:T(8,128)(2,1)}, u32[]{:S(2)}) copy-start(bf16[128,4096]{1,0:T(8,128)(2,1)} %get-tuple-element.16) | copy-start | bytes 3145732
  91.3 3.8 %copy-start.10 = (bf16[1024,128]{1,0:T(8,128)(2,1)S(1)}, bf16[1024,128]{1,0:T(8,128)(2,1)}, u32[]{:S(2)}) copy-start(bf16[1024,128]{1,0:T(8,128)(2,1)} %get-tuple-element.20) | copy-start | bytes 786436
  91.3 3.8 %copy-start.13 = (bf16[1024,128]{1,0:T(8,128)(2,1)S(1)}, bf16[1024,128]{1,0:T(8,128)(2,1)}, u32[]{:S(2)}) copy-start(bf16[1024,128]{1,0:T(8,128)(2,1)} %get-tuple-element.19) | copy-start | bytes 786436
  96.9 2.5 %copy-start.12 = (bf16[1024,128]{1,0:T(8,128)(2,1)S(1)}, bf16[1024,128]{1,0:T(8,128)(2,1)}, u32[]{:S(2)}) copy-start(bf16[1024,128]{1,0:T(8,128)(2,1)} %get-tuple-element.18) | copy-start | bytes 786436
  99.4 1.5 copy-start.11
  134.2 5.8 %copy-start.9 = (bf16[128,1024]{1,0:T(8,128)(2,1)S(1)}, bf16[128,1024]{1,0:T(8,128)(2,1)}, u32[]{:S(2)}) copy-start(bf16[128,1024]{1,0:T(8,128)(2,1)} %get-tuple-element.22) | copy-start | bytes 786436
  140.1 6.4 %copy-start.8 = (bf16[128,1024]{1,0:T(8,128)(2,1)S(1)}, bf16[128,1024]{1,0:T(8,128)(2,1)}, u32[]{:S(2)}) copy-start(bf16[128,1024]{1,0:T(8,128)(2,1)} %get-tuple-element.23) | copy-start | bytes 786436
  140.1 12.9 %slice-start.4 = ((s8[8388608]{0:T(1024)(128)(4,1)}), s8[4194304]{0:T(1024)(128)(4,1)S(1)}, s32[]{:S(2)}) async-start(s8[8388608]{0:T(1024)(128)(4,1)} %bitcast.47), calls=%async_computation.4 | async-start | bytes 8388608
  146.5 6.5 %slice-start.5 = ((s8[8388608]{0:T(1024)(128)(4,1)}), s8[4194304]{0:T(1024)(128)(4,1)S(1)}, s32[]{:S(2)}) async-start(s8[8388608]{0:T(1024)(128)(4,1)} %bitcast.47), calls=%async_computation.5 | async-start | bytes 8388608
  146.5 6.5 %copy-start.2 = (bf16[128,4096]{1,0:T(8,128)(2,1)S(1)}, bf16[128,4096]{1,0:T(8,128)(2,1)}, u32[]{:S(2)}) copy-start(bf16[128,4096]{1,0:T(8,128)(2,1)} %get-tuple-element.15) | copy-start | bytes 3145732
  146.5 6.5 %copy-start.7 = (bf16[128,1024]{1,0:T(8,128)(2,1)S(1)}, bf16[128,1024]{1,0:T(8,128)(2,1)}, u32[]{:S(2)}) copy-start(bf16[128,1024]{1,0:T(8,128)(2,1)} %get-tuple-element.24) | copy-start | bytes 786436
  157.0 32.1 %copy-start.3 = (bf16[128,1024]{1,0:T(8,128)(2,1)S(1)}, bf16[128,1024]{1,0:T(8,128)(2,1)}, u32[]{:S(2)}) copy-start(bf16[128,1024]{1,0:T(8,128)(2,1)} %convolution_convert_fusion.2.refs_0_) | copy-start | bytes 786436
  157.0 32.1 %dynamic-slice-start = ((f32[4096]{0:T(1024)}, s32[]{:T(128)}), f32[1024]{0:T(1024)S(1)}, s32[]{:S(2)}) async-start(f32[4096]{0:T(1024)} %param.12, s32[]{:T(128)} %select_n.30), calls=%async_computation.8 | async-start | bytes 8704 | tf_op jit(solution)/shard_map/dynamic_slice | solution.py:383
  157.0 32.2 %copy-start.6 = (bf16[128,1024]{1,0:T(8,128)(2,1)S(1)}, bf16[128,1024]{1,0:T(8,128)(2,1)}, u32[]{:S(2)}) copy-start(bf16[128,1024]{1,0:T(8,128)(2,1)} %param.17) | copy-start | bytes 786436
